TPU v7x, 32 devices: a whole 2x2x4 slice. The times are simulated.
32 devices in a mesh: ep: 8 (over z, x), tp: 4 (over y, core).
Axes of the slice: x: 2, y: 2, z: 4, core: 2. Of those that a mesh axis runs over, the one named last changes fastest.
Arguments:
- hidden: bfloat16 [512, 2880], P('ep'), may hold values from -0.59765625 to 0.59765625
- queries: bfloat16 [512, 2048], P('ep', 'tp'), may hold values from -160 to 160
- new_keys: bfloat16 [512, 256], P('ep', 'tp'), may hold values from -6 to 6
- new_values: bfloat16 [512, 256], P('ep', 'tp'), may hold values from -6 to 6
- key_cache: bfloat16 [64, 4, 64, 1024], P('ep', 'tp'), may hold values from -6 to 6
- value_cache: bfloat16 [64, 4, 64, 1024], P('ep', 'tp'), may hold values from -6 to 6
- cache_lengths: int32 [64], P('ep'), may hold values from 16 to 1024
- w_out: bfloat16 [2048, 2880], P('tp'), may hold values from -0.125 to 0.125
- w_router: bfloat16 [2880, 8], replicated, may hold values from -0.109375 to 0.109375
- routes: int32 [512, 4], P('ep'), may hold values from 0 to 7, all different within a row; in each aligned block of 16 rows (0 to 15, 16 to 31, ...) at most 16 rows name the same one
- w_gate: bfloat16 [8, 2880, 1536], P('ep', None, 'tp'), may hold values from -0.109375 to 0.109375
- w_up: bfloat16 [8, 2880, 1536], P('ep', None, 'tp'), may hold values from -0.109375 to 0.109375
- w_down: bfloat16 [8, 1536, 2880], P('ep', 'tp'), may hold values from -0.15625 to 0.15625
Outputs:
- layer_out: bfloat16 [512, 2880], P(('ep', 'tp'))
Inputs may be any that keep to these rules, and one draw needn't show every extreme that they name: `routes`: each token names 4 different experts; in each aligned block of 16 tokens no expert is named by more than 16 tokens, and in some blocks one expert is named by exactly 16.
All inputs are finite; a program needn't handle non-finite values.
Results may differ from a plain program's by a relative error of at most 0.02.
Values may be sent and summed in bfloat16 or wider, within the bound.
A program may use at most 64 MiB of HBM per device.

v0:
```python
import functools

import jax
import jax.numpy as jnp
from jax import lax
from jax.experimental import pallas as pl
from jax.experimental.pallas import tpu as pltpu
from jax.sharding import PartitionSpec as P

LANES = 128
MESH = pl.DeviceIdType.MESH


def attend(queries, new_keys, new_values, key_cache, value_cache, cache_lengths):
    seq_count, kv_count, head_dim, length = key_cache.shape
    new_count = queries.shape[0] // seq_count
    group_size = queries.shape[1] // (kv_count * head_dim)
    row_count = new_count * group_size
    scale = head_dim ** (-0.5)
    query_block = queries.reshape(seq_count, new_count, kv_count, group_size, head_dim)
    query_block = query_block.transpose(0, 2, 1, 3, 4).reshape(
        seq_count, kv_count, row_count, head_dim
    )
    fresh_keys = new_keys.reshape(seq_count, new_count, kv_count, head_dim).transpose(0, 2, 1, 3)
    fresh_values = new_values.reshape(seq_count, new_count, kv_count, head_dim).transpose(
        0, 2, 1, 3
    )
    cache_scores = (
        jnp.einsum("skrd,skdl->skrl", query_block, key_cache, preferred_element_type=jnp.float32)
        * scale
    )
    in_cache = jnp.arange(length)[None, :] < cache_lengths[:, None]
    cache_scores = jnp.where(in_cache[:, None, None, :], cache_scores, -1e30)
    fresh_scores = (
        jnp.einsum("skrd,sknd->skrn", query_block, fresh_keys, preferred_element_type=jnp.float32)
        * scale
    )
    causal = (jnp.arange(row_count) // group_size)[:, None] >= jnp.arange(new_count)[None, :]
    fresh_scores = jnp.where(causal[None, None, :, :], fresh_scores, -1e30)
    row_max = jnp.maximum(
        jnp.max(cache_scores, -1, keepdims=True), jnp.max(fresh_scores, -1, keepdims=True)
    )
    cache_exp = jnp.exp(cache_scores - row_max)
    fresh_exp = jnp.exp(fresh_scores - row_max)
    denom_sum = jnp.sum(cache_exp, -1, keepdims=True) + jnp.sum(fresh_exp, -1, keepdims=True)
    cache_probs = (cache_exp / denom_sum).astype(jnp.bfloat16)
    fresh_probs = (fresh_exp / denom_sum).astype(jnp.bfloat16)
    head_mix = jnp.einsum(
        "skrl,skdl->skrd", cache_probs, value_cache, preferred_element_type=jnp.float32
    )
    head_mix = head_mix + jnp.einsum(
        "skrn,sknd->skrd", fresh_probs, fresh_values, preferred_element_type=jnp.float32
    )
    head_mix = head_mix.reshape(seq_count, kv_count, new_count, group_size, head_dim).transpose(
        0, 2, 1, 3, 4
    )
    return head_mix.reshape(seq_count * new_count, kv_count * group_size * head_dim).astype(
        jnp.bfloat16
    )


def expert_apply(received, w_gate, w_up, w_down):
    width = received.shape[-1]
    flat_rows = received.reshape(-1, width)
    gate_proj = jnp.dot(flat_rows, w_gate[0], preferred_element_type=jnp.float32)
    up_proj = jnp.dot(flat_rows, w_up[0], preferred_element_type=jnp.float32)
    activated = ((up_proj + 1.0) * gate_proj * jax.nn.sigmoid(1.702 * gate_proj)).astype(
        jnp.bfloat16
    )
    partial_out = jnp.dot(activated, w_down[0], preferred_element_type=jnp.float32)
    return partial_out.reshape(received.shape[0], received.shape[1], width)


def layer_kernel(
    ep_size,
    experts,
    part_ref,
    hidden_ref,
    router_ref,
    routes_ref,
    gate_hbm,
    up_hbm,
    down_hbm,
    out_ref,
    got,
    res,
    rows,
    mixed,
    core_in,
    b_in,
    a_in,
    z_in,
    w_gate,
    w_up,
    w_down,
    router,
    load_sem,
    first_send,
    first_recv,
    gather_send,
    gather_recv,
    core_send,
    core_recv,
    sum_send,
    sum_recv,
):
    tp_size, block_rows, width = part_ref.shape
    padded = rows.shape[2]
    base = width // LANES * LANES
    offset = width - base
    line = ep_size // 2
    lane_slots = 4 * line
    ep = lax.axis_index("ep")
    tp = lax.axis_index("tp")
    x = ep % 2
    z = ep // 2
    core = tp % 2
    y = tp // 2
    x_step = 1 - 2 * x
    y_step = 2 - 4 * y
    partner = (ep, tp + 1 - 2 * core)
    a_dev = (ep + (1 - core) * x_step, tp + core * y_step)
    b_dev = (ep + core * x_step, tp + (1 - core) * y_step)

    def z_dev(k):
        return (((z + k) % line) * 2 + x, tp)

    loads = [
        pltpu.make_async_copy(gate_hbm.at[0], w_gate.at[pl.ds(0, width)], load_sem.at[0]),
        pltpu.make_async_copy(up_hbm.at[0], w_up.at[pl.ds(0, width)], load_sem.at[1]),
        pltpu.make_async_copy(down_hbm.at[0], w_down, load_sem.at[2]),
    ]
    for load in loads:
        load.start()

    peers = [(ep, (tp + k) % tp_size) for k in range(1, tp_size)]
    peers += [(ep + x_step, tp)] + [z_dev(k) for k in range(1, line)]
    barrier = pltpu.get_barrier_semaphore()
    for peer in peers:
        pl.semaphore_signal(barrier, inc=1, device_id=peer, device_id_type=MESH)
    pl.semaphore_wait(barrier, len(peers))

    def send(src, dst, send_sem, recv_sem, index, device):
        copy = pltpu.make_async_remote_copy(
            src_ref=src,
            dst_ref=dst,
            send_sem=send_sem.at[index],
            recv_sem=recv_sem.at[index],
            device_id=device,
            device_id_type=MESH,
        )
        copy.start()
        return copy

    firsts = []
    for k in (2, 1, 3):
        target = (tp + k) % tp_size
        firsts.append(
            send(part_ref.at[target], got.at[k - 1], first_send, first_recv, k - 1, (ep, target))
        )
    w_gate[width:, :] = jnp.zeros((padded - width, w_gate.shape[1]), w_gate.dtype)
    w_up[width:, :] = jnp.zeros((padded - width, w_up.shape[1]), w_up.dtype)
    router[...] = jnp.zeros(router.shape, router.dtype)
    router[offset : offset + experts, :width] = router_ref[...]
    router[offset + experts : offset + 2 * experts, :width] = router_ref[...]
    res[:, base:] = jnp.zeros((block_rows, padded - base), jnp.float32)
    own = part_ref[tp].astype(jnp.float32)
    for copy in firsts:
        copy.wait_recv()
    for k in range(tp_size - 1):
        own = own + got[k].astype(jnp.float32)
    mine = pl.ds(pl.multiple_of(tp * block_rows, block_rows), block_rows)
    own = own.astype(jnp.bfloat16).astype(jnp.float32) + hidden_ref[mine, :].astype(jnp.float32)
    res[:, :width] = own
    scale = lax.rsqrt(jnp.sum(own * own, -1, keepdims=True) * (1.0 / width) + 1e-05)
    normed = (res[...] * scale).astype(jnp.bfloat16)
    logits = lax.dot_general(
        normed, router[...], (((1,), (1,)), ((), ())), preferred_element_type=jnp.float32
    )
    lane = lax.broadcasted_iota(jnp.int32, (block_rows, LANES), 1)
    second = lane >= offset + experts
    lane_expert = jnp.where(second, lane - offset - experts, lane - offset)
    routes = routes_ref[mine, :]
    named = lane_expert == routes[:, 0:1]
    for r in range(1, routes.shape[1]):
        named = named | (lane_expert == routes[:, r : r + 1])
    picked_exp = jnp.where(named, jnp.exp(logits), 0.0)
    denom = jnp.sum(jnp.where(second, 0.0, picked_exp), -1, keepdims=True)
    weights = picked_exp / denom
    high = weights.astype(jnp.bfloat16).astype(jnp.float32)
    tail = jnp.where(second, weights - high, high)
    tail = jnp.where(lane < offset, normed[:, base:].astype(jnp.float32), tail)
    rows[0, :, :base] = normed[:, :base]
    rows[0, :, base:] = tail.astype(jnp.bfloat16)

    moves = {}

    def spread(slot, device, source):
        moves[slot] = send(
            rows.at[source], rows.at[slot], gather_send, gather_recv, slot, device
        )

    def forward(slot):
        if slot < line:
            spread(line + slot, a_dev, slot)
        if slot < 2 * line:
            spread(2 * line + slot, b_dev, slot)
        spread(lane_slots + slot, partner, slot)

    near = [k for k in range(1, line) if k in (1, line - 1)]
    far = [k for k in range(1, line) if k not in near]
    order = near + far
    for k in order:
        spread(line - k, z_dev(k), 0)
    forward(0)
    for slot in [line - k for k in order] + list(range(line, 2 * line)):
        moves[slot].wait_recv()
        forward(slot)
    for load in loads:
        load.wait()
    share_lane = lax.broadcasted_iota(jnp.int32, (2 * line * block_rows, LANES), 1)
    chosen = (share_lane == offset + ep) | (share_lane == offset + experts + ep)

    def expert(start):
        count = 2 * line
        held = rows[start : start + count].reshape(count * block_rows, padded)
        gate = jnp.dot(held, w_gate[...], preferred_element_type=jnp.float32)
        up = jnp.dot(held, w_up[...], preferred_element_type=jnp.float32)
        active = ((up + 1.0) * gate * jax.nn.sigmoid(1.702 * gate)).astype(jnp.bfloat16)
        share = jnp.sum(
            jnp.where(chosen, held[:, base:].astype(jnp.float32), 0.0), -1, keepdims=True
        )
        step = 6 * LANES
        for low in range(0, width, step):
            size = min(step, width - low)
            out = lax.dot_general(
                active,
                w_down[low : low + size, :],
                (((1,), (1,)), ((), ())),
                preferred_element_type=jnp.float32,
            )
            mixed[start : start + count, :, low : low + size] = (
                (share * out).astype(jnp.bfloat16).reshape(count, block_rows, size)
            )

    half = 2 * line
    crossing = {}
    sums = {}

    def cross(quarter):
        crossing[quarter] = send(
            mixed.at[pl.ds(lane_slots + quarter * line, line)],
            core_in.at[pl.ds(quarter * line, line)],
            core_send,
            core_recv,
            quarter,
            partner,
        )

    def reduce_send(slot, parts, dst, device):
        total = mixed[slot].astype(jnp.float32) + core_in[slot].astype(jnp.float32)
        for part in parts:
            total = total + part.astype(jnp.float32)
        mixed[slot] = total.astype(jnp.bfloat16)
        sums[slot] = send(mixed.at[slot], dst, sum_send, sum_recv, slot, device)

    expert(0)
    for slot in range(half):
        moves[lane_slots + slot].wait_recv()
    expert(lane_slots)
    cross(1)
    cross(0)
    for slot in range(half, 2 * half):
        moves[slot].wait_recv()
        forward(slot)
    crossing[1].wait_recv()
    for slot in range(line, half):
        reduce_send(slot, [], a_in.at[slot - line], a_dev)
    for slot in range(half, 2 * half):
        moves[lane_slots + slot].wait_recv()
    expert(lane_slots + half)
    cross(3)
    cross(2)
    expert(half)
    crossing[3].wait_recv()
    for slot in range(3 * line, 4 * line):
        reduce_send(slot, [], a_in.at[slot - half], a_dev)
    crossing[2].wait_recv()
    for slot in range(half, 3 * line):
        sums[line + slot].wait_recv()
        reduce_send(slot, [a_in[slot - line]], b_in.at[slot - half], b_dev)
    crossing[0].wait_recv()
    for slot in far + near:
        sums[line + slot].wait_recv()
        sums[half + slot].wait_recv()
        reduce_send(slot, [b_in[slot], a_in[slot]], z_in.at[slot - 1], z_dev(slot))
    sums[half].wait_recv()
    sums[line].wait_recv()
    total = res[:, :width] + mixed[0].astype(jnp.float32) + core_in[0].astype(jnp.float32)
    total = total + b_in[0].astype(jnp.float32) + a_in[0].astype(jnp.float32)
    for slot in far + near:
        sums[slot].wait_recv()
        total = total + z_in[slot - 1].astype(jnp.float32)
    out_ref[...] = total.astype(jnp.bfloat16)
    for copy in (
        firsts + list(moves.values()) + list(crossing.values()) + list(sums.values())
    ):
        copy.wait_send()


def fused_layer(partial_value, hidden, w_router, routes, w_gate, w_up, w_down):
    ep_size = lax.axis_size("ep")
    tp_size = lax.axis_size("tp")
    width = hidden.shape[1]
    block_rows = hidden.shape[0] // tp_size
    experts = w_router.shape[1]
    hidden_share = w_gate.shape[2]
    base = width // LANES * LANES
    padded = base + LANES
    line = ep_size // 2
    slots = 8 * line
    vmem = pl.BlockSpec(memory_space=pltpu.VMEM)
    any_space = pl.BlockSpec(memory_space=pl.ANY)
    dma = pltpu.SemaphoreType.DMA
    bf16 = jnp.bfloat16
    return pl.pallas_call(
        functools.partial(layer_kernel, ep_size, experts),
        out_shape=jax.ShapeDtypeStruct((block_rows, width), bf16),
        in_specs=[vmem] * 4 + [any_space] * 3,
        out_specs=vmem,
        scratch_shapes=[
            pltpu.VMEM((tp_size - 1, block_rows, width), bf16),
            pltpu.VMEM((block_rows, padded), jnp.float32),
            pltpu.VMEM((slots, block_rows, padded), bf16),
            pltpu.VMEM((slots, block_rows, width), bf16),
            pltpu.VMEM((slots // 2, block_rows, width), bf16),
            pltpu.VMEM((slots // 8, block_rows, width), bf16),
            pltpu.VMEM((slots // 4, block_rows, width), bf16),
            pltpu.VMEM((line - 1, block_rows, width), bf16),
            pltpu.VMEM((padded, hidden_share), bf16),
            pltpu.VMEM((padded, hidden_share), bf16),
            pltpu.VMEM((width, hidden_share), bf16),
            pltpu.VMEM((LANES, padded), bf16),
            dma((3,)),
            dma((tp_size - 1,)),
            dma((tp_size - 1,)),
            dma((slots,)),
            dma((slots,)),
            dma((4,)),
            dma((4,)),
            dma((slots // 2,)),
            dma((slots // 2,)),
        ],
        compiler_params=pltpu.CompilerParams(
            collective_id=0, has_side_effects=True, vmem_limit_bytes=67043328
        ),
    )(
        partial_value.reshape(tp_size, block_rows, width),
        hidden,
        w_router.T,
        routes,
        w_gate,
        w_up,
        jnp.swapaxes(w_down, 1, 2),
    )


def body(
    hidden,
    queries,
    new_keys,
    new_values,
    key_cache,
    value_cache,
    cache_lengths,
    w_out,
    w_router,
    routes,
    w_gate,
    w_up,
    w_down,
):
    tp_size = lax.axis_size("tp")
    tp_index = lax.axis_index("tp")
    width = hidden.shape[1]
    block_rows = hidden.shape[0] // tp_size
    top_count = routes.shape[1]
    experts = w_router.shape[1]
    capacity = min(block_rows, max(2, (2 * block_rows * top_count + experts - 1) // experts))
    start_row = tp_index * block_rows
    attended = attend(queries, new_keys, new_values, key_cache, value_cache, cache_lengths)
    partial_value = jnp.dot(attended, w_out, preferred_element_type=jnp.float32)
    fits = width % LANES + 2 * experts <= LANES and experts == lax.axis_size("ep")
    if capacity >= block_rows and tp_size == 4 and experts % 2 == 0 and experts > 2 and fits:
        return fused_layer(
            partial_value.astype(jnp.bfloat16),
            hidden,
            w_router,
            routes,
            w_gate,
            w_up,
            w_down,
        )
    summed = lax.psum_scatter(
        partial_value.astype(jnp.bfloat16), "tp", scatter_dimension=0, tiled=True
    ).astype(jnp.float32)
    residual = (
        lax.dynamic_slice_in_dim(hidden, start_row, block_rows, 0).astype(jnp.float32) + summed
    )
    local_routes = lax.dynamic_slice_in_dim(routes, start_row, block_rows, 0)
    block_count = 1
    normed = (
        residual * lax.rsqrt(jnp.mean(residual * residual, -1, keepdims=True) + 1e-05)
    ).astype(jnp.bfloat16)
    logits = jnp.dot(normed, w_router, preferred_element_type=jnp.float32)
    expert_ids = jnp.arange(experts, dtype=jnp.int32)
    matches = local_routes[:, :, None] == expert_ids[None, None, :]
    picked = jnp.sum(jnp.where(matches, logits[:, None, :], 0.0), -1)
    picked_exp = jnp.exp(picked)
    weights = picked_exp / jnp.sum(picked_exp, -1, keepdims=True)
    flat_routes = local_routes.reshape(-1)
    one_hot = (
        flat_routes.reshape(block_count, block_rows * top_count)[:, :, None]
        == expert_ids[None, None, :]
    ).astype(jnp.int32)
    slot_rank = jnp.sum((jnp.cumsum(one_hot, 1) - one_hot) * one_hot, -1)
    slot_index = (
        slot_rank + (jnp.arange(block_count, dtype=jnp.int32) * capacity)[:, None]
    ).reshape(-1)
    outgoing = jnp.zeros((experts, block_count * capacity, width), jnp.bfloat16)
    outgoing = outgoing.at[flat_routes, slot_index].set(jnp.repeat(normed, top_count, axis=0))
    grouped = expert_apply(
        lax.all_gather(
            lax.all_to_all(outgoing, "ep", split_axis=0, concat_axis=0, tiled=True),
            "tp",
            axis=1,
            tiled=True,
        ),
        w_gate,
        w_up,
        w_down,
    )
    group_total = lax.psum_scatter(
        grouped.astype(jnp.bfloat16), "tp", scatter_dimension=1, tiled=True
    ).astype(jnp.float32)
    returned = lax.all_to_all(
        group_total.astype(jnp.bfloat16), "ep", split_axis=0, concat_axis=0, tiled=True
    ).astype(group_total.dtype)
    routed = returned[flat_routes, slot_index].reshape(-1, top_count, width)
    mixture = jnp.sum(weights[:, :, None] * routed, 1)
    return (residual + mixture).astype(jnp.bfloat16)


def solution(mesh):
    return jax.shard_map(
        body,
        mesh=mesh,
        in_specs=(
            P("ep", None),
            P("ep", "tp"),
            P("ep", "tp"),
            P("ep", "tp"),
            P("ep", "tp", None, None),
            P("ep", "tp", None, None),
            P("ep"),
            P("tp", None),
            P(),
            P("ep", None),
            P("ep", None, "tp"),
            P("ep", None, "tp"),
            P("ep", "tp", None),
        ),
        out_specs=P(("ep", "tp"), None),
        check_vma=False,
    )
```

profile of v0, /device:TPU:0, one launch (start us, length us, event | category | flops | bytes accessed | tf_op | source)
XLA Modules:
  0.0 66.1 jit_solution(10801764956049345897)
XLA Ops:
  0.0 0.0 copy-start.2
  0.0 0.7 %iota_compare_fusion = pred[8,1024]{1,0:T(8,128)(4,1)S(1)} fusion(s32[8]{0:T(128)} %param.19), kind=kLoop, calls=%fused_computation.17 | loop fusion | flops 8192 | bytes 8224 | tf_op jit(solution)/shard_map/lt | solution.py:32
  0.7 1.0 %reshape.131 = bf16[8,64,64]{2,1,0:T(8,128)(2,1)S(1)} reshape(bf16[64,512]{1,0:T(8,128)(2,1)} %param.14) | data formatting | bytes 131072 | tf_op jit(solution)/shard_map/reshape.2
  1.7 0.0 copy-start.4
  1.7 1.8 %fusion = (f32[8,64]{1,0:T(8,128)S(1)}, f32[8,64,1024]{2,1,0:T(8,128)S(1)}) fusion(pred[8,1024]{1,0:T(8,128)(4,1)S(1)} %iota_compare_fusion, bf16[8,64,64]{2,1,0:T(8,128)(2,1)S(1)} %reshape.131, bf16[8,1,64,1024]{3,2,1,0:T(8,128)(2,1)} %param.17), kind=kOutput, calls=%fused_computation.4 | convolution fusion | flops 68681216 | bytes 3221504 | tf_op jit(solution)/shard_map/skrd,skdl->skrl/dot_general | solution.py:29
  3.6 0.0 copy-done.2
  3.6 0.2 fusion.16
  3.8 0.6 fusion.1
  4.5 0.0 copy-done.4
  4.5 0.0 copy-start.1
  4.5 0.0 copy-start
  4.5 0.7 %fusion.4 = f32[8,64,64]{2,1,0:T(8,128)S(1)} fusion(bf16[8,1,64,1024]{3,2,1,0:T(8,128)(2,1)S(1)} %copy-done.4, f32[8,64,1024]{2,1,0:T(8,128)S(1)} %get-tuple-element.6, f32[8,64]{1,0:T(8,128)S(1)} %add.17, f32[8,64]{1,0:T(8,128)S(1)} %max.8, pred[8,1024]{1,0:T(8,128)(4,1)S(1)} %iota_compare_fusion), kind=kOutput, calls=%fused_computation.10 | convolution fusion | flops 69730304 | bytes 3289088 | tf_op jit(solution)/shard_map/skrl,skdl->skrd/dot_general | solution.py:48
  5.3 0.0 copy-done.1
  5.3 0.0 copy-start.3
  5.3 0.2 fusion.2
  5.5 0.1 convert_element_type.20
  5.7 0.7 copy-done
  6.3 1.7 %convolution_convert_fusion = bf16[64,2880]{1,0:T(8,128)(2,1)} fusion(bf16[64,512]{1,0:T(8,128)(2,1)S(1)} %convert_element_type.20, bf16[512,2880]{0,1:T(8,128)(2,1)S(1)} %copy-done), kind=kOutput, calls=%fused_computation | convolution fusion | flops 188928000 | bytes 3383296 | tf_op jit(solution)/shard_map/dot_general | solution.py:392
  8.1 0.0 copy-done.3
  8.1 0.7 %copy.14.routes_ref = s32[64,4]{1,0:T(8,128)} copy(s32[64,4]{0,1:T(4,128)S(1)} %copy-done.3) | data formatting | bytes 2048 | tf_op args[9]
  8.8 55.8 %shard_map.127 = bf16[16,2880]{1,0:T(8,128)(2,1)} custom-call(bf16[4,16,2880]{2,1,0:T(8,128)(2,1)} %bitcast.24, bf16[64,2880]{1,0:T(8,128)(2,1)} %hidden_ref.1, bf16[8,2880]{1,0:T(8,128)(2,1)} %bitcast.25, s32[64,4]{1,0:T(8,128)} %copy.14.routes_ref, bf16[1,2880,384]{2,1,0:T(8,128)(2,1)} %gate_hbm.1, bf16[1,2880,384]{2,1,0:T(8,128)(2,1)} %up_hbm.1, ...), custom_call_target="tpu_custom_call" | custom-call | tf_op jit(solution)/shard_map/pallas_call | solution.py:326
  64.6 1.5 %copy.16 = bf16[16,2880]{1,0:T(8,128)(2,1)} copy(bf16[16,2880]{1,0:T(8,128)(2,1)} %shard_map.127) | data formatting | bytes 184320
  (5 shorter events, 0.0 us)
Async XLA Ops:
  0.0 3.6 %copy-start.2 = (bf16[64,64]{1,0:T(8,128)(2,1)S(1)}, bf16[64,64]{1,0:T(8,128)(2,1)}, u32[]{:S(2)}) copy-start(bf16[64,64]{1,0:T(8,128)(2,1)} %param.15) | copy-start | bytes 24580
  1.7 2.8 %copy-start.4 = (bf16[8,1,64,1024]{3,2,1,0:T(8,128)(2,1)S(1)}, bf16[8,1,64,1024]{3,2,1,0:T(8,128)(2,1)}, u32[]{:S(2)}) copy-start(bf16[8,1,64,1024]{3,2,1,0:T(8,128)(2,1)} %param.18) | copy-start | bytes 3145732
  4.5 0.8 %copy-start.1 = (bf16[64,64]{1,0:T(8,128)(2,1)S(1)}, bf16[64,64]{1,0:T(8,128)(2,1)}, u32[]{:S(2)}) copy-start(bf16[64,64]{1,0:T(8,128)(2,1)} %param.16) | copy-start | bytes 24580
  4.5 1.8 %copy-start = (bf16[512,2880]{0,1:T(8,128)(2,1)S(1)}, bf16[512,2880]{0,1:T(8,128)(2,1)}, u32[]{:S(2)}) copy-start(bf16[512,2880]{0,1:T(8,128)(2,1)} %param.20) | copy-start | bytes 8847364
  5.3 2.8 %copy-start.3 = (s32[64,4]{0,1:T(4,128)S(1)}, s32[64,4]{0,1:T(4,128)}, u32[]{:S(2)}) copy-start(s32[64,4]{0,1:T(4,128)} %param.22) | copy-start | bytes 3076
where the time goes:
time: 66.5 us; the launch traced here: 66.1 us
  Pallas kernels  55.8 us (84%)
  matrix products  4.75 us (7%)
  local copies, waits for them, and re-layouts  4.05 us (6%)
  other arithmetic  1.41 us (2%)
    pallas_call x1, Pallas kernels, fused_layer(): pl.pallas_call(functools.partial(layer_kernel, ep_size, experts), out_sha...  55.8 us
    unnamed x12, local copies, waits for them, and re-layouts  2.93 us
    dot_general x1, matrix products, attend(): jnp.einsum('skrd,skdl->skrl', query_block, key_cache, preferred_element_t...  1.84 us
    dot_general x1, matrix products, body(): partial_value = jnp.dot(attended, w_out, preferred_element_type=jnp.float32)  1.74 us

commit v1 on v0

v1 whole, which is shorter than its diff:
```python
import functools

import jax
import jax.numpy as jnp
from jax import lax
from jax.experimental import pallas as pl
from jax.experimental.pallas import tpu as pltpu
from jax.sharding import PartitionSpec as P

LANES = 128
LOG2E = 1.4426950408889634
MESH = pl.DeviceIdType.MESH


def attend(queries, new_keys, new_values, key_cache, value_cache, cache_lengths):
    seq_count, kv_count, head_dim, length = key_cache.shape
    new_count = queries.shape[0] // seq_count
    group_size = queries.shape[1] // (kv_count * head_dim)
    row_count = new_count * group_size
    scale = head_dim ** (-0.5)
    query_block = queries.reshape(seq_count, new_count, kv_count, group_size, head_dim)
    query_block = query_block.transpose(0, 2, 1, 3, 4).reshape(
        seq_count, kv_count, row_count, head_dim
    )
    fresh_keys = new_keys.reshape(seq_count, new_count, kv_count, head_dim).transpose(0, 2, 1, 3)
    fresh_values = new_values.reshape(seq_count, new_count, kv_count, head_dim).transpose(
        0, 2, 1, 3
    )
    cache_scores = (
        jnp.einsum("skrd,skdl->skrl", query_block, key_cache, preferred_element_type=jnp.float32)
        * scale
    )
    in_cache = jnp.arange(length)[None, :] < cache_lengths[:, None]
    cache_scores = jnp.where(in_cache[:, None, None, :], cache_scores, -1e30)
    fresh_scores = (
        jnp.einsum("skrd,sknd->skrn", query_block, fresh_keys, preferred_element_type=jnp.float32)
        * scale
    )
    causal = (jnp.arange(row_count) // group_size)[:, None] >= jnp.arange(new_count)[None, :]
    fresh_scores = jnp.where(causal[None, None, :, :], fresh_scores, -1e30)
    row_max = jnp.maximum(
        jnp.max(cache_scores, -1, keepdims=True), jnp.max(fresh_scores, -1, keepdims=True)
    )
    cache_exp = jnp.exp(cache_scores - row_max)
    fresh_exp = jnp.exp(fresh_scores - row_max)
    denom_sum = jnp.sum(cache_exp, -1, keepdims=True) + jnp.sum(fresh_exp, -1, keepdims=True)
    cache_probs = (cache_exp / denom_sum).astype(jnp.bfloat16)
    fresh_probs = (fresh_exp / denom_sum).astype(jnp.bfloat16)
    head_mix = jnp.einsum(
        "skrl,skdl->skrd", cache_probs, value_cache, preferred_element_type=jnp.float32
    )
    head_mix = head_mix + jnp.einsum(
        "skrn,sknd->skrd", fresh_probs, fresh_values, preferred_element_type=jnp.float32
    )
    head_mix = head_mix.reshape(seq_count, kv_count, new_count, group_size, head_dim).transpose(
        0, 2, 1, 3, 4
    )
    return head_mix.reshape(seq_count * new_count, kv_count * group_size * head_dim).astype(
        jnp.bfloat16
    )


def expert_apply(received, w_gate, w_up, w_down):
    width = received.shape[-1]
    flat_rows = received.reshape(-1, width)
    gate_proj = jnp.dot(flat_rows, w_gate[0], preferred_element_type=jnp.float32)
    up_proj = jnp.dot(flat_rows, w_up[0], preferred_element_type=jnp.float32)
    activated = ((up_proj + 1.0) * gate_proj * jax.nn.sigmoid(1.702 * gate_proj)).astype(
        jnp.bfloat16
    )
    partial_out = jnp.dot(activated, w_down[0], preferred_element_type=jnp.float32)
    return partial_out.reshape(received.shape[0], received.shape[1], width)


def layer_kernel(
    ep_size,
    experts,
    lens_hbm,
    query_hbm,
    new_key_hbm,
    new_value_hbm,
    key_hbm,
    value_hbm,
    w_out_hbm,
    hidden_hbm,
    router_hbm,
    routes_hbm,
    gate_hbm,
    up_hbm,
    down_hbm,
    out_ref,
    lens,
    query,
    query_wide,
    fresh_key,
    fresh_value,
    keys,
    values,
    w_out,
    hidden,
    router,
    routes,
    named_all,
    attended,
    part,
    got,
    res,
    rows,
    mixed,
    core_in,
    a_in,
    b_in,
    z_in,
    w_gate,
    w_up,
    w_down,
    load_sem,
    seq_sem,
    first_send,
    first_recv,
    line_send,
    gather_send,
    gather_recv,
    core_send,
    core_recv,
    sum_send,
    a_recv,
    b_recv,
    z_recv,
):
    tp_size, block_rows, width = part.shape
    padded = rows.shape[2]
    base = width // LANES * LANES
    offset = width - base
    line = ep_size // 2
    pair = 2 * line
    unit = 4 * line
    seq_count, head_dim, length = keys.shape
    tokens, query_width = query.shape
    new_count = tokens // seq_count
    seq_block = block_rows // new_count
    cut = (padded // LANES + 1) // 2 * LANES
    bf16 = jnp.bfloat16
    f32 = jnp.float32
    ep = lax.axis_index("ep")
    tp = lax.axis_index("tp")
    x = ep % 2
    z = ep // 2
    core = tp % 2
    y = tp // 2
    x_step = 1 - 2 * x
    y_step = 2 - 4 * y
    mate = tp + 1 - 2 * core
    partner = (ep, mate)
    a_dev = (ep + (1 - core) * x_step, tp + core * y_step)
    b_dev = (ep + core * x_step, tp + (1 - core) * y_step)

    by_distance = [sorted(range(line), key=lambda p: (abs(p - q), p)) for q in range(line)]

    def near(k):
        place = by_distance[0][k] + 0 * z
        for q in range(1, line):
            place = jnp.where(z == q, by_distance[q][k], place)
        return place

    planes = [z] + [near(k) for k in range(1, line)]
    order = [(tp + 2) % tp_size, (mate + 2) % tp_size, mate, tp]

    def block_of(index):
        return pl.ds(pl.multiple_of(index * block_rows, block_rows), block_rows)

    def load(src, dst, index):
        copy = pltpu.make_async_copy(src, dst, load_sem.at[index])
        copy.start()
        return copy

    small = [load(lens_hbm, lens, 0)]
    cache = []
    for i, source in enumerate(order):
        seqs = pl.ds(source * seq_block, seq_block)
        held = pl.ds(i * seq_block, seq_block)
        there = pl.ds(i * block_rows, block_rows)
        moved = []
        for j, (src, dst) in enumerate(
            (
                (query_hbm.at[block_of(source)], query.at[there]),
                (new_key_hbm.at[block_of(source)], fresh_key.at[there]),
                (new_value_hbm.at[block_of(source)], fresh_value.at[there]),
                (key_hbm.at[seqs, 0], keys.at[held]),
                (value_hbm.at[seqs, 0], values.at[held]),
            )
        ):
            copy = pltpu.make_async_copy(src, dst, seq_sem.at[i, j])
            copy.start()
            moved.append(copy)
        cache.append(moved)
    w_out_load = load(w_out_hbm, w_out, 1)
    small.append(load(routes_hbm, routes, 2))
    side = [
        load(hidden_hbm.at[block_of(tp)], hidden, 3),
        load(router_hbm, router.at[pl.ds(0, experts)], 4),
    ]

    peers = [(ep, (tp + k) % tp_size) for k in range(1, tp_size)]
    peers += [(ep + x_step, tp)]
    peers += [(planes[k] * 2 + x, tp) for k in range(1, line)]
    barrier = pltpu.get_barrier_semaphore()
    for peer in peers:
        pl.semaphore_signal(barrier, inc=1, device_id=peer, device_id_type=MESH)

    def send(src, dst, send_sem, recv_sem, device):
        copy = pltpu.make_async_remote_copy(
            src_ref=src,
            dst_ref=dst,
            send_sem=send_sem,
            recv_sem=recv_sem,
            device_id=device,
            device_id_type=MESH,
        )
        copy.start()
        return copy

    for moved in cache:
        for copy in moved:
            copy.wait()
    experts_load = [
        load(gate_hbm.at[0], w_gate.at[pl.ds(0, width)], 5),
        load(up_hbm.at[0], w_up.at[pl.ds(0, width)], 6),
        load(down_hbm.at[0], w_down, 7),
    ]
    for copy in small:
        copy.wait()
    twice = (
        lax.broadcasted_iota(jnp.int32, (head_dim, LANES), 1) % head_dim
        == lax.broadcasted_iota(jnp.int32, (head_dim, LANES), 0)
    ).astype(bf16)
    key_twice = jnp.dot(fresh_key[...], twice, preferred_element_type=f32).astype(bf16)
    value_twice = jnp.dot(fresh_value[...], twice, preferred_element_type=f32).astype(bf16)
    query_wide[...] = query[...].astype(f32)
    group_size = query_width // head_dim
    seq_rows = group_size * new_count
    factor = head_dim**-0.5 * LOG2E
    low_half = lax.broadcasted_iota(jnp.int32, (new_count, LANES), 1) < head_dim
    place = lax.broadcasted_iota(jnp.int32, (seq_rows, length), 1)
    fresh_lane = lax.broadcasted_iota(jnp.int32, (seq_rows, tokens), 1)
    fresh_row = lax.broadcasted_iota(jnp.int32, (seq_rows, tokens), 0) % new_count
    columns = (((1,), (1,)), ((), ()))

    def attend_sequence(s):
        size = lens[order[s // seq_block] * seq_block + s % seq_block]
        mine = slice(s * new_count, (s + 1) * new_count)
        pieces = []
        for low in range(0, query_width, LANES):
            both = query_wide[mine, low : low + LANES]
            pieces += [jnp.where(low_half, both, 0.0), jnp.where(low_half, 0.0, both)]
        left = jnp.concatenate(pieces, axis=0).astype(bf16)
        key = keys[s]
        scores = jnp.dot(left, jnp.concatenate([key, key], axis=0), preferred_element_type=f32)
        scores = jnp.where(place < size, scores * factor, -1e30)
        fresh = lax.dot_general(left, key_twice, columns, preferred_element_type=f32)
        admitted = (fresh_lane >= s * new_count) & (fresh_lane <= s * new_count + fresh_row)
        fresh = jnp.where(admitted, fresh * factor, -1e30)
        top = jnp.maximum(
            jnp.max(scores, -1, keepdims=True), jnp.max(fresh, -1, keepdims=True)
        )
        scores = jnp.exp2(scores - top)
        fresh = jnp.exp2(fresh - top)
        total = jnp.sum(scores, -1, keepdims=True) + jnp.sum(fresh, -1, keepdims=True)
        value = values[s]
        out = lax.dot_general(
            scores.astype(bf16),
            jnp.concatenate([value, value], axis=0),
            columns,
            preferred_element_type=f32,
        )
        out = out + jnp.dot(fresh.astype(bf16), value_twice, preferred_element_type=f32)
        out = out / total
        for i, low in enumerate(range(0, query_width, LANES)):
            first = out[2 * i * new_count : (2 * i + 1) * new_count]
            second = out[(2 * i + 1) * new_count : (2 * i + 2) * new_count]
            attended[mine, low : low + LANES] = jnp.where(low_half, first, second)

    step = 6 * LANES

    def project(first):
        left = attended[first * block_rows : (first + 2) * block_rows].astype(bf16)
        for low in range(0, width, step):
            size = min(step, width - low)
            out = lax.dot_general(
                left, w_out[low : low + size, :], columns, preferred_element_type=f32
            )
            part[first, :, low : low + size] = out[:block_rows].astype(bf16)
            if first == 0:
                part[1, :, low : low + size] = out[block_rows:].astype(bf16)
            else:
                res[:, low : low + size] = out[block_rows:]

    firsts = []

    def first_hop(i):
        firsts.append(
            send(part.at[i], got.at[i], first_send.at[i], first_recv.at[i], (ep, order[i]))
        )

    for s in range(2 * seq_block):
        attend_sequence(s)
    w_out_load.wait()
    project(0)
    pl.semaphore_wait(barrier, len(peers))
    first_hop(0)
    first_hop(1)
    for s in range(2 * seq_block, 4 * seq_block):
        attend_sequence(s)
    project(2)
    first_hop(2)

    for copy in side:
        copy.wait()
    w_gate[width:, :] = jnp.zeros((padded - width, w_gate.shape[1]), bf16)
    w_up[width:, :] = jnp.zeros((padded - width, w_up.shape[1]), bf16)
    res[:, width:] = jnp.zeros((block_rows, padded - width), f32)
    weight_in = router[:experts, :width]
    router_wide = jnp.concatenate(
        [
            jnp.zeros((offset, width), bf16),
            weight_in,
            weight_in,
            jnp.zeros((LANES - offset - 2 * experts, width), bf16),
        ],
        axis=0,
    )
    lane = lax.broadcasted_iota(jnp.int32, (block_rows, LANES), 1)
    second = lane >= offset + experts
    chosen_by = jnp.zeros((experts, tokens), jnp.bool_)
    expert_row = lax.broadcasted_iota(jnp.int32, (experts, tokens), 0)
    for r in range(routes.shape[0]):
        chosen_by = chosen_by | (expert_row == routes[r : r + 1, :])
    lane_row = lax.broadcasted_iota(jnp.int32, (experts, LANES), 1) - offset
    expert_lane = lax.broadcasted_iota(jnp.int32, (experts, LANES), 0)
    spread_to = (lane_row == expert_lane) | (lane_row == expert_lane + experts)
    named_all[...] = lax.dot_general(
        chosen_by.astype(f32),
        spread_to.astype(f32),
        (((0,), (0,)), ((), ())),
        preferred_element_type=f32,
    )
    named = named_all[block_of(tp), :] > 0.5
    own = res[:, :width] + hidden[...].astype(f32)
    for i in (2, 0, 1):
        firsts[i].wait_recv()
        own = own + got[i].astype(f32)
    res[:, :width] = own
    scale = lax.rsqrt(jnp.sum(own * own, -1, keepdims=True) * (1.0 / width) + 1e-05)

    def slot(kind, quarter, plane):
        return (quarter // 2) * unit + kind * pair + (quarter % 2) * line + plane

    def half(h, end):
        return pl.ds(0, cut) if h == 0 else pl.ds(cut, end - cut)

    def row_copy(src, dst, h, send_sem, device):
        return pltpu.make_async_remote_copy(
            src_ref=rows.at[src, :, half(h, padded)],
            dst_ref=rows.at[dst, :, half(h, padded)],
            send_sem=send_sem,
            recv_sem=gather_recv.at[dst, h],
            device_id=device,
            device_id_type=MESH,
        )

    def line_copies(k, h):
        plane = planes[k]
        here = slot(0, 0, plane)
        up = (plane <= z) & (z < line - 1)
        down = (plane >= z) & (z > 0)
        return (
            (up, row_copy(here, here, h, line_send.at[0, k, h], (ep + 2, tp))),
            (down, row_copy(here, here, h, line_send.at[1, k, h], (ep - 2, tp))),
        )

    sent = []

    def hop(src, dst, h, device):
        copy = row_copy(src, dst, h, gather_send.at[dst, h], device)
        copy.start()
        sent.append(copy)

    def forward(quarter, k, h):
        plane = planes[k]
        here = slot(0, quarter, plane)
        if quarter == 0:
            for wanted, copy in line_copies(k, h):
                pl.when(wanted)(copy.start)
            hop(here, slot(0, 1, plane), h, a_dev)
            hop(here, slot(0, 2, plane), h, b_dev)
        if quarter == 1:
            hop(here, slot(0, 3, plane), h, b_dev)
        hop(here, slot(1, quarter, plane), h, partner)

    def arrive(kind, quarter, k, h):
        here = slot(kind, quarter, planes[k])
        row_copy(here, here, h, gather_send.at[here, h], partner).wait_recv()

    mine = slot(0, 0, z)
    rows[mine, :, :cut] = (res[:, :cut] * scale).astype(bf16)
    forward(0, 0, 0)
    normed = (res[...] * scale).astype(bf16)
    logits = lax.dot_general(
        normed[:, :width], router_wide, columns, preferred_element_type=f32
    )
    picked_exp = jnp.where(named, jnp.exp(logits), 0.0)
    denom = jnp.sum(jnp.where(second, 0.0, picked_exp), -1, keepdims=True)
    weights = picked_exp / denom
    high = weights.astype(bf16).astype(f32)
    tail = jnp.where(second, weights - high, high)
    tail = jnp.where(lane < offset, normed[:, base:].astype(f32), tail)
    rows[mine, :, cut:base] = normed[:, cut:base]
    rows[mine, :, base:] = tail.astype(bf16)
    forward(0, 0, 1)

    early = []
    for k in range(line):
        if k + 1 < line:
            early += [(1, k, 0), (0, k + 1, 0), (1, k, 1), (0, k + 1, 1)]
        else:
            early += [(1, k, 0), (1, k, 1)]
        if k == 0:
            early += [(2, 0, 0), (2, 0, 1)]
        if k > 0 and k + 1 < line:
            early += [(2, k, 0), (2, k, 1), (3, k - 1, 0), (3, k - 1, 1)]
    late = [
        (q, k, h)
        for k in range(line)
        for q in (2, 3)
        for h in (0, 1)
        if (q, k, h) not in early
    ]
    for quarter, k, h in early:
        arrive(0, quarter, k, h)
        forward(quarter, k, h)

    share_lane = lax.broadcasted_iota(jnp.int32, (unit * block_rows, LANES), 1)
    chosen = (share_lane == offset + ep) | (share_lane == offset + experts + ep)
    crossing = {}

    def cross(u, h):
        crossing[u, h] = send(
            mixed.at[pl.ds(u * unit + pair, pair), :, half(h, width)],
            core_in.at[pl.ds(u * pair, pair), :, half(h, width)],
            core_send.at[u, h],
            core_recv.at[u, h],
            partner,
        )

    def expert(u):
        start = u * unit
        held = rows[start : start + unit].reshape(unit * block_rows, padded)
        gate = jnp.dot(held, w_gate[...], preferred_element_type=f32)
        up = jnp.dot(held, w_up[...], preferred_element_type=f32)
        active = ((up + 1.0) * gate * jax.nn.sigmoid(1.702 * gate)).astype(bf16)
        share = jnp.sum(jnp.where(chosen, held[:, base:].astype(f32), 0.0), -1, keepdims=True)
        for h, (first, last) in enumerate(((0, cut), (cut, width))):
            for low in range(first, last, step):
                size = min(step, last - low)
                out = lax.dot_general(
                    active, w_down[low : low + size, :], columns, preferred_element_type=f32
                )
                mixed[start : start + unit, :, low : low + size] = (
                    (share * out).astype(bf16).reshape(unit, block_rows, size)
                )
            cross(u, h)

    for copy in experts_load:
        copy.wait()
    for quarter in (0, 1):
        for k in range(line):
            for h in (0, 1):
                arrive(1, quarter, k, h)
    expert(0)
    for quarter, k, h in late:
        arrive(0, quarter, k, h)
        forward(quarter, k, h)

    sums = []

    def total_of(quarter, k, h, parts):
        plane = planes[k]
        there = (quarter // 2) * pair + (quarter % 2) * line + plane
        columns_of = half(h, width)
        total = mixed[slot(0, quarter, plane), :, columns_of].astype(f32)
        total = total + core_in[there, :, columns_of].astype(f32)
        for buffer, index in parts:
            total = total + buffer[index, :, columns_of].astype(f32)
        return total

    def reduce_send(quarter, k, h, parts, dst, recv_sem, device):
        here = slot(0, quarter, planes[k])
        columns_of = half(h, width)
        mixed[here, :, columns_of] = total_of(quarter, k, h, parts).astype(bf16)
        sums.append(
            send(
                mixed.at[here, :, columns_of],
                dst.at[:, columns_of],
                sum_send.at[quarter, k, h],
                recv_sem,
                device,
            )
        )

    def landed(dst, recv_sem):
        pltpu.make_async_remote_copy(
            src_ref=dst,
            dst_ref=dst,
            send_sem=sum_send.at[0, 0, 0],
            recv_sem=recv_sem,
            device_id=partner,
            device_id_type=MESH,
        ).wait_recv()

    far = list(range(line - 1, -1, -1))

    def send_a(quarter, k, h):
        index = (quarter // 2) * line + planes[k]
        reduce_send(quarter, k, h, [], a_in.at[index], a_recv.at[index, h], a_dev)

    def send_b(k, h):
        index = line + planes[k]
        landed(a_in.at[index, :, half(h, width)], a_recv.at[index, h])
        reduce_send(2, k, h, [(a_in, index)], b_in.at[planes[k]], b_recv.at[planes[k], h], b_dev)

    def gathered(k, h):
        plane = planes[k]
        landed(a_in.at[plane, :, half(h, width)], a_recv.at[plane, h])
        landed(b_in.at[plane, :, half(h, width)], b_recv.at[plane, h])
        return [(a_in, plane), (b_in, plane)]

    def send_z(k, h):
        device = (planes[k] * 2 + x, tp)
        reduce_send(0, k, h, gathered(k, h), z_in.at[z], z_recv.at[z, h], device)

    for h in (0, 1):
        crossing[0, h].wait_recv()
    for k in far:
        for h in (0, 1):
            send_a(1, k, h)
    for quarter in (2, 3):
        for k in range(line):
            for h in (0, 1):
                arrive(1, quarter, k, h)
    expert(1)
    for h in (0, 1):
        crossing[1, h].wait_recv()
    for k in far:
        for h in (0, 1):
            send_a(3, k, h)
    second_hop = [(k, h) for k in far for h in (0, 1)]
    last_hop = [(k, h) for k in far[:-1] for h in (0, 1)]
    lead = 5
    for i, (k, h) in enumerate(second_hop):
        send_b(k, h)
        if i + 1 >= lead and last_hop:
            send_z(*last_hop.pop(0))
    for k, h in last_hop:
        send_z(k, h)
    for h in (0, 1):
        columns_of = half(h, width)
        total = res[:, columns_of] + total_of(0, 0, h, gathered(0, h))
        for k in far[:-1]:
            landed(z_in.at[planes[k], :, columns_of], z_recv.at[planes[k], h])
            total = total + z_in[planes[k], :, columns_of].astype(f32)
        out_ref[:, columns_of] = total.astype(bf16)
    for copy in firsts + sent + list(crossing.values()) + sums:
        copy.wait_send()
    for k in range(line):
        for h in (0, 1):
            for wanted, copy in line_copies(k, h):
                pl.when(wanted)(copy.wait_send)


def fused_layer(
    hidden,
    queries,
    new_keys,
    new_values,
    key_cache,
    value_cache,
    cache_lengths,
    w_out,
    w_router,
    routes,
    w_gate,
    w_up,
    w_down,
):
    ep_size = lax.axis_size("ep")
    tp_size = lax.axis_size("tp")
    tokens, width = hidden.shape
    block_rows = tokens // tp_size
    experts = w_router.shape[1]
    hidden_share = w_gate.shape[2]
    base = width // LANES * LANES
    padded = base + LANES
    line = ep_size // 2
    slots = 8 * line
    seq_count, _, head_dim, length = key_cache.shape
    query_width = queries.shape[1]
    any_space = pl.BlockSpec(memory_space=pl.ANY)
    dma = pltpu.SemaphoreType.DMA
    bf16 = jnp.bfloat16
    f32 = jnp.float32
    vmem = pltpu.VMEM
    return pl.pallas_call(
        functools.partial(layer_kernel, ep_size, experts),
        out_shape=jax.ShapeDtypeStruct((block_rows, width), bf16),
        in_specs=[any_space] * 13,
        out_specs=pl.BlockSpec(memory_space=pltpu.VMEM),
        scratch_shapes=[
            pltpu.SMEM((seq_count,), jnp.int32),
            vmem((tokens, query_width), bf16),
            vmem((tokens, query_width), f32),
            vmem((tokens, head_dim), bf16),
            vmem((tokens, head_dim), bf16),
            vmem((seq_count, head_dim, length), bf16),
            vmem((seq_count, head_dim, length), bf16),
            vmem((width, query_width), bf16),
            vmem((block_rows, width), bf16),
            vmem((experts, width), bf16),
            vmem((routes.shape[1], tokens), jnp.int32),
            vmem((tokens, LANES), f32),
            vmem((tokens, query_width), f32),
            vmem((tp_size, block_rows, width), bf16),
            vmem((tp_size - 1, block_rows, width), bf16),
            vmem((block_rows, padded), f32),
            vmem((slots, block_rows, padded), bf16),
            vmem((slots, block_rows, width), bf16),
            vmem((slots // 2, block_rows, width), bf16),
            vmem((2 * line, block_rows, width), bf16),
            vmem((line, block_rows, width), bf16),
            vmem((line, block_rows, width), bf16),
            vmem((padded, hidden_share), bf16),
            vmem((padded, hidden_share), bf16),
            vmem((width, hidden_share), bf16),
            dma((8,)),
            dma((tp_size, 5)),
            dma((tp_size - 1,)),
            dma((tp_size - 1,)),
            dma((2, line, 2)),
            dma((slots, 2)),
            dma((slots, 2)),
            dma((2, 2)),
            dma((2, 2)),
            dma((4, line, 2)),
            dma((2 * line, 2)),
            dma((line, 2)),
            dma((line, 2)),
        ],
        compiler_params=pltpu.CompilerParams(
            collective_id=0, has_side_effects=True, vmem_limit_bytes=67043328
        ),
    )(
        cache_lengths,
        queries,
        new_keys,
        new_values,
        key_cache,
        value_cache,
        w_out.T,
        hidden,
        w_router.T,
        routes.T,
        w_gate,
        w_up,
        jnp.swapaxes(w_down, 1, 2),
    )


def body(
    hidden,
    queries,
    new_keys,
    new_values,
    key_cache,
    value_cache,
    cache_lengths,
    w_out,
    w_router,
    routes,
    w_gate,
    w_up,
    w_down,
):
    tp_size = lax.axis_size("tp")
    tp_index = lax.axis_index("tp")
    width = hidden.shape[1]
    block_rows = hidden.shape[0] // tp_size
    top_count = routes.shape[1]
    experts = w_router.shape[1]
    capacity = min(block_rows, max(2, (2 * block_rows * top_count + experts - 1) // experts))
    start_row = tp_index * block_rows
    fits = width % LANES + 2 * experts <= LANES and experts == lax.axis_size("ep")
    seq_count, kv_count, head_dim, _ = key_cache.shape
    new_count = hidden.shape[0] // seq_count
    fits = fits and kv_count == 1 and 2 * head_dim == LANES and new_count == 8
    fits = fits and block_rows == 2 * new_count
    if capacity >= block_rows and tp_size == 4 and experts % 2 == 0 and experts > 2 and fits:
        return fused_layer(
            hidden,
            queries,
            new_keys,
            new_values,
            key_cache,
            value_cache,
            cache_lengths,
            w_out,
            w_router,
            routes,
            w_gate,
            w_up,
            w_down,
        )
    attended = attend(queries, new_keys, new_values, key_cache, value_cache, cache_lengths)
    partial_value = jnp.dot(attended, w_out, preferred_element_type=jnp.float32)
    summed = lax.psum_scatter(
        partial_value.astype(jnp.bfloat16), "tp", scatter_dimension=0, tiled=True
    ).astype(jnp.float32)
    residual = (
        lax.dynamic_slice_in_dim(hidden, start_row, block_rows, 0).astype(jnp.float32) + summed
    )
    local_routes = lax.dynamic_slice_in_dim(routes, start_row, block_rows, 0)
    block_count = 1
    normed = (
        residual * lax.rsqrt(jnp.mean(residual * residual, -1, keepdims=True) + 1e-05)
    ).astype(jnp.bfloat16)
    logits = jnp.dot(normed, w_router, preferred_element_type=jnp.float32)
    expert_ids = jnp.arange(experts, dtype=jnp.int32)
    matches = local_routes[:, :, None] == expert_ids[None, None, :]
    picked = jnp.sum(jnp.where(matches, logits[:, None, :], 0.0), -1)
    picked_exp = jnp.exp(picked)
    weights = picked_exp / jnp.sum(picked_exp, -1, keepdims=True)
    flat_routes = local_routes.reshape(-1)
    one_hot = (
        flat_routes.reshape(block_count, block_rows * top_count)[:, :, None]
        == expert_ids[None, None, :]
    ).astype(jnp.int32)
    slot_rank = jnp.sum((jnp.cumsum(one_hot, 1) - one_hot) * one_hot, -1)
    slot_index = (
        slot_rank + (jnp.arange(block_count, dtype=jnp.int32) * capacity)[:, None]
    ).reshape(-1)
    outgoing = jnp.zeros((experts, block_count * capacity, width), jnp.bfloat16)
    outgoing = outgoing.at[flat_routes, slot_index].set(jnp.repeat(normed, top_count, axis=0))
    grouped = expert_apply(
        lax.all_gather(
            lax.all_to_all(outgoing, "ep", split_axis=0, concat_axis=0, tiled=True),
            "tp",
            axis=1,
            tiled=True,
        ),
        w_gate,
        w_up,
        w_down,
    )
    group_total = lax.psum_scatter(
        grouped.astype(jnp.bfloat16), "tp", scatter_dimension=1, tiled=True
    ).astype(jnp.float32)
    returned = lax.all_to_all(
        group_total.astype(jnp.bfloat16), "ep", split_axis=0, concat_axis=0, tiled=True
    ).astype(group_total.dtype)
    routed = returned[flat_routes, slot_index].reshape(-1, top_count, width)
    mixture = jnp.sum(weights[:, :, None] * routed, 1)
    return (residual + mixture).astype(jnp.bfloat16)


def solution(mesh):
    return jax.shard_map(
        body,
        mesh=mesh,
        in_specs=(
            P("ep", None),
            P("ep", "tp"),
            P("ep", "tp"),
            P("ep", "tp"),
            P("ep", "tp", None, None),
            P("ep", "tp", None, None),
            P("ep"),
            P("tp", None),
            P(),
            P("ep", None),
            P("ep", None, "tp"),
            P("ep", None, "tp"),
            P("ep", "tp", None),
        ),
        out_specs=P(("ep", "tp"), None),
        check_vma=False,
    )
```

time: 66.5 us -> 58.4 us (0.88)
  matrix products: 4.75 us -> 0 us
  local copies, waits for them, and re-layouts: 4.05 us -> 1.54 us
  other arithmetic: 1.41 us -> 0 us
  Pallas kernels: 55.8 us -> 56.6 us
    dot_general x5 -> x0, matrix products: 4.75 us -> none  [the longest x1 1.84 us: attend(): jnp.einsum('skrd,skdl->skrl', query_block, key_cache, preferred_element_t...]
    unnamed x12 -> x1, local copies, waits for them, and re-layouts: 2.93 us -> 1.54 us
    another operation x1 -> x0, local copies, waits for them, and re-layouts: 0.98 us -> none
    pallas_call x1, Pallas kernels: 55.8 us -> 56.6 us  [fused_layer(): pl.pallas_call(functools.partial(layer_kernel, ep_size, experts), out_sha...]
    lt x1 -> x0, other arithmetic: 0.74 us -> none  [attend(): in_cache = jnp.arange(length)[None, :] < cache_lengths[:, None]]
where the time goes in v1:
time: 58.4 us; the launch traced here: 58.2 us
  Pallas kernels  56.6 us (97%)
  local copies, waits for them, and re-layouts  1.54 us (3%)
    pallas_call x1, Pallas kernels, fused_layer(): pl.pallas_call(functools.partial(layer_kernel, ep_size, experts), out_sha...  56.6 us
    unnamed x1, local copies, waits for them, and re-layouts  1.54 us

profile of v1, /device:TPU:0, one launch (start us, length us, event | category | flops | bytes accessed | tf_op | source)
XLA Modules:
  0.0 58.2 jit_solution(7648768128097196844)
XLA Ops:
  0.0 56.6 %shard_map.127 = bf16[16,2880]{1,0:T(8,128)(2,1)} custom-call(s32[8]{0:T(128)} %lens_hbm.1, bf16[64,512]{1,0:T(8,128)(2,1)} %query_hbm.1, bf16[64,64]{1,0:T(8,128)(2,1)} %new_key_hbm.1, bf16[64,64]{1,0:T(8,128)(2,1)} %new_value_hbm.1, bf16[8,1,64,1024]{3,2,1,0:T(8,128)(2,1)} %key_hbm.1, bf16[8,1,64,1024]{3,2,1,0:T(8,128)(2,1)} %value_hbm.1, ...), custom_call_target="tpu_custom_call" | custom-call | tf_op jit(solution)/shard_map/pallas_call | solution.py:612
  56.6 1.5 %copy.15 = bf16[16,2880]{1,0:T(8,128)(2,1)} copy(bf16[16,2880]{1,0:T(8,128)(2,1)} %shard_map.127) | data formatting | bytes 184320
